TPU v7x, 32 devices: a whole 2x2x4 slice. The times are simulated.
32 devices in a mesh: dp: 4 (over x, core), seq: 4 (over z), tensor: 2 (over y).
Axes of the slice: x: 2, y: 2, z: 4, core: 2. Of those that a mesh axis runs over, the one named last changes fastest.
Arguments:
- vit_out: bfloat16 [4096, 3200], P(('dp', 'seq')), may hold values from -6 to 6
- ln_gain: float32 [3200], replicated, may hold values from 0.1 to 1.9
- ln_bias: float32 [3200], replicated, may hold values from -3 to 3
- proj_weight: bfloat16 [3200, 4, 2048], P(None, None, 'tensor'), may hold values from -0.109375 to 0.109375
- proj_bias: float32 [4, 2048], P(None, 'tensor'), may hold values from -3 to 3
- text_embed: bfloat16 [16384, 8192], P('dp', ('seq', 'tensor')), may hold values from -6 to 6
- norm_gain: float32 [8192], P(('seq', 'tensor')), may hold values from 0.1 to 1.9
- tile_dest: int32 [32, 1], replicated, may hold values from 0 to 3; in each aligned block of 8 rows (0 to 7, 8 to 15, ...) at most 4 rows name the same one
- tile_place: int32 [4, 32], replicated, may hold values from 0 to 31, each once within a row
Outputs:
- normed: bfloat16 [16384, 8192], P('dp', ('seq', 'tensor'))
Inputs may be any that keep to these rules, and one draw needn't show every extreme that they name: `tile_dest`: in each aligned block of 8 rows (one encoder group's tiles) no replica is named more than 4 times, a bound that some block reaches. `tile_place`: each row is a permutation of 0 to 31.
All inputs are finite; a program needn't handle non-finite values.
Results may differ from a plain program's by a relative error of at most 0.0048.
Values may be sent and summed in bfloat16 or wider, within the bound.
A program may use at most 128 MiB of HBM per device.

v0:
```python
import jax
import jax.numpy as jnp
from jax import lax
from jax.sharding import PartitionSpec as P

D = 8192
TILE = 128


def layer_norm(rows, ln_gain, ln_bias):
    values = rows.astype(jnp.float32)
    center = values - jnp.mean(values, axis=-1, keepdims=True)
    spread = jnp.mean(center * center, axis=-1, keepdims=True)
    return (center * lax.rsqrt(spread + 1e-06) * ln_gain + ln_bias).astype(jnp.bfloat16)


def arrival_ranks(destination, replicas):
    onehot = (destination[:, None] == jnp.arange(replicas, dtype=jnp.int32)[None, :]).astype(
        jnp.int32
    )
    before = jnp.cumsum(onehot, axis=0) - onehot
    return jnp.sum(before * onehot, axis=1)


def row_squares(rows):
    values = rows.astype(jnp.float32)
    return jnp.sum(values * values, axis=-1)


def local(
    vit_out, ln_gain, ln_bias, proj_weight, proj_bias, text_embed, norm_gain, tile_dest, tile_place
):
    replicas = lax.axis_size("dp")
    owners = lax.axis_size("seq")
    my_replica = lax.axis_index("dp")
    local_rows = vit_out.shape[0]
    width_in = vit_out.shape[1]
    column_block = proj_weight.shape[2]
    positions = tile_place.shape[1]
    seq_rows = text_embed.shape[0]
    group_tiles = owners * local_rows // TILE
    total_tiles = tile_dest.shape[0]
    normed_in = layer_norm(vit_out, ln_gain, ln_bias)
    weights_flat = proj_weight.reshape(width_in, owners * column_block)
    hidden = jnp.dot(
        normed_in, weights_flat, preferred_element_type=jnp.float32
    ) + proj_bias.reshape(-1)
    projected = hidden.astype(jnp.bfloat16)
    regrouped = lax.all_to_all(
        projected.reshape(local_rows, owners, column_block),
        "seq",
        split_axis=1,
        concat_axis=0,
        tiled=True,
    )
    group_rows = regrouped.reshape(owners * local_rows, column_block)
    destination = tile_dest[:, 0]
    ranks = arrival_ranks(destination, replicas)
    place_row = lax.dynamic_index_in_dim(tile_place, my_replica, 0, keepdims=False)
    slot_of_tile = jnp.where(
        destination == my_replica, jnp.take(place_row, jnp.minimum(ranks, positions - 1)), -1
    )
    matches = slot_of_tile[None, :] == jnp.arange(positions, dtype=jnp.int32)[:, None]
    source_tile = (
        jnp.sum(
            matches.astype(jnp.int32) * (jnp.arange(total_tiles, dtype=jnp.int32) + 1)[None, :],
            axis=1,
        )
        - 1
    )
    text_tiles = text_embed.reshape(positions, TILE, column_block)
    capacity = max(2, 2 * group_tiles // replicas)
    local_dest = lax.dynamic_slice_in_dim(destination, my_replica * group_tiles, group_tiles)
    local_rank = arrival_ranks(local_dest, replicas)
    slot_index = local_dest * capacity + local_rank
    filling = slot_index[None, :] == jnp.arange(replicas * capacity, dtype=jnp.int32)[:, None]
    slot_source = (
        jnp.sum(
            filling.astype(jnp.int32) * (jnp.arange(group_tiles, dtype=jnp.int32) + 1)[None, :],
            axis=1,
        )
        - 1
    )
    tiles = group_rows.reshape(group_tiles, TILE, column_block)
    outgoing = jnp.where(
        (slot_source >= 0)[:, None, None],
        tiles[jnp.clip(slot_source, 0, group_tiles - 1)],
        jnp.zeros((), jnp.bfloat16),
    )
    outgoing = outgoing.reshape(replicas, capacity, TILE, column_block)
    incoming = lax.all_to_all(outgoing, "dp", split_axis=0, concat_axis=0, tiled=True).reshape(
        replicas * capacity, TILE, column_block
    )
    group_ranks = jax.vmap(lambda block: arrival_ranks(block, replicas))(
        destination.reshape(replicas, group_tiles)
    ).reshape(-1)
    safe_tile = jnp.clip(source_tile, 0, total_tiles - 1)
    arrival_index = safe_tile // group_tiles * capacity + jnp.take(group_ranks, safe_tile)
    picked = incoming[jnp.clip(arrival_index, 0, replicas * capacity - 1)]
    assembled = jnp.where((source_tile >= 0)[:, None, None], picked, text_tiles).reshape(
        seq_rows, column_block
    )
    squares = row_squares(assembled)
    totals = lax.psum(squares, ("seq", "tensor"))
    scale = lax.rsqrt(totals / D + 1e-05)
    return (assembled.astype(jnp.float32) * scale[:, None] * norm_gain).astype(jnp.bfloat16)


def solution(mesh):
    placed = (
        P(("dp", "seq"), None),
        P(),
        P(),
        P(None, None, "tensor"),
        P(None, "tensor"),
        P("dp", ("seq", "tensor")),
        P(("seq", "tensor")),
        P(),
        P(),
    )
    return jax.shard_map(
        local, mesh=mesh, in_specs=placed, out_specs=P("dp", ("seq", "tensor")), check_vma=False
    )
```

profile of v0, /device:TPU:0, one launch (start us, length us, event | category | flops | bytes accessed | tf_op | source)
XLA Modules:
  0.0 208.4 jit_solution(405158420390305600)
XLA Ops:
  0.0 0.0 copy-start
  0.0 0.0 copy-start.2
  0.0 0.0 copy-start.1
  0.0 0.0 copy-start.5
  0.0 0.0 copy-start.6
  0.0 18.2 %copy.13 = bf16[400,8,4,1024]{3,1,2,0:T(8,128)(2,1)} copy(bf16[400,8,4,1024]{3,2,1,0:T(4,128)(2,1)} %bitcast.39) | data formatting | bytes 52428800
  18.2 0.0 copy-done.2
  18.2 0.0 copy-done.1
  18.3 0.3 convert_reduce_fusion
  18.6 0.6 fusion.6
  19.2 0.0 copy-done.5
  19.2 0.0 copy-done.6
  19.2 12.3 %fusion.3 = bf16[256,4096]{1,0:T(8,128)(2,1)S(1)} fusion(bf16[3200,4096]{1,0:T(8,128)(2,1)} %bitcast.40, f32[4096]{0:T(1024)S(1)} %bitcast.46, bf16[256,3200]{1,0:T(8,128)(2,1)S(1)} %copy-done.1, f32[3200]{0:T(1024)S(1)} %copy-done.5, f32[3200]{0:T(1024)S(1)} %copy-done.6, f32[256]{0:T(256)S(1)} %add_rsqrt_fusion.1, f32[256]{0:T(256)S(1)} %broadcast_multiply_fusion), kind=kOutput, calls=%fused_computation.11 | convolution fusion | flops 6717898752 | bytes 29993984 | tf_op jit(solution)/shard_map/dot_general | solution.py:45
  31.5 0.0 copy-start.3
  31.5 1.5 copy.17
  33.0 6.4 %all-to-all-start = ((bf16[256,4,1024]{2,0,1:T(8,128)(2,1)}), bf16[256,4,1024]{2,0,1:T(8,128)(2,1)S(1)}, u32[]{:S(2)}, u32[]{:S(2)}) async-start(bf16[256,4,1024]{2,0,1:T(8,128)(2,1)} %bitcast.43), calls=%async_computation | async-start | bytes 4194304 | tf_op jit(solution)/shard_map/all_to_all | solution.py:49
  39.4 0.0 copy-done.3
  39.4 0.1 dynamic-slice_bitcast_fusion
  39.5 0.2 reduce_window_sum.34
  39.7 0.1 iota_add_fusion
  39.8 0.1 select_reduce_fusion.3
  39.9 0.1 ge.24
  40.0 47.6 %all-to-all-done = bf16[256,4,1024]{2,0,1:T(8,128)(2,1)S(1)} async-done(((bf16[256,4,1024]{2,0,1:T(8,128)(2,1)}), bf16[256,4,1024]{2,0,1:T(8,128)(2,1)S(1)}, u32[]{:S(2)}, u32[]{:S(2)}) %all-to-all-start) | async-done | bytes 2097184 | tf_op jit(solution)/shard_map/all_to_all | solution.py:49
  87.6 2.8 %gather_fusion = bf16[16,128,1024]{2,1,0:T(8,128)(2,1)} fusion(bf16[8,128,1024]{2,1,0:T(8,128)(2,1)S(1)} %bitcast.41, s32[1024]{0:T(1024)S(1)} %pad_clamp_fusion.2), kind=kCustom, calls=%fused_computation.2 | custom fusion | bytes 8388672 | tf_op jit(solution)/shard_map/gather | solution.py:87
  90.4 4.5 %broadcast_select_fusion = bf16[4,4,128,1024]{3,2,1,0:T(8,128)(2,1)} fusion(bf16[4,4,128,1024]{3,2,1,0:T(8,128)(2,1)} %bitcast.42, pred[4,4]{1,0:T(4,128)(4,1)S(1)} %ge.24), kind=kLoop, calls=%fused_computation.12 | loop fusion | flops 2097152 | bytes 8388624 | tf_op jit(solution)/shard_map/jit(_where)/select_n | solution.py:85
  95.0 4.9 %all-to-all-start.1 = ((bf16[4,4,128,1024]{3,2,1,0:T(8,128)(2,1)}), bf16[4,4,128,1024]{3,2,1,0:T(8,128)(2,1)}, u32[]{:S(2)}, u32[]{:S(2)}) async-start(bf16[4,4,128,1024]{3,2,1,0:T(8,128)(2,1)} %broadcast_select_fusion), calls=%async_computation.1 | async-start | bytes 8388608 | tf_op jit(solution)/shard_map/all_to_all | solution.py:91
  99.9 0.6 broadcast.200
  100.5 0.7 reduce.3
  101.2 0.1 eq.87
  101.3 0.7 reduce_window_sum.35
  102.0 0.1 reshape.103
  102.1 0.1 fusion.15
  102.2 0.1 reduce_window_sum.33
  102.2 0.0 copy-done
  102.3 0.2 select_reduce_fusion.1
  102.5 0.7 gather_fusion.2
  103.2 0.1 select_reduce_fusion
  103.3 0.7 gather_fusion.3
  104.1 0.1 broadcast_bitcast_fusion
  104.1 43.9 %all-to-all-done.1 = bf16[4,4,128,1024]{3,2,1,0:T(8,128)(2,1)} async-done(((bf16[4,4,128,1024]{3,2,1,0:T(8,128)(2,1)}), bf16[4,4,128,1024]{3,2,1,0:T(8,128)(2,1)}, u32[]{:S(2)}, u32[]{:S(2)}) %all-to-all-start.1) | async-done | bytes 4194336 | tf_op jit(solution)/shard_map/all_to_all | solution.py:91
  148.1 7.1 %gather_fusion.1 = bf16[32,128,1024]{2,1,0:T(8,128)(2,1)} fusion(bf16[16,128,1024]{2,1,0:T(8,128)(2,1)} %bitcast.10, s32[1024]{0:T(1024)S(1)} %pad_clamp_fusion), kind=kCustom, calls=%fused_computation.3 | custom fusion | bytes 16777344 | tf_op jit(solution)/shard_map/gather | solution.py:99
  155.2 0.0 copy-start.4
  155.2 7.7 %fusion = f32[4096]{0:T(1024)S(1)} fusion(bf16[4096,1024]{1,0:T(8,128)(2,1)} %param.16, bf16[32,128,1024]{2,1,0:T(8,128)(2,1)} %gather_fusion.1, pred[4096]{0:T(1024)(128)(4,1)S(1)} %broadcast_bitcast_fusion), kind=kLoop, calls=%fused_computation.6 | loop fusion | flops 16773120 | bytes 16797696 | tf_op jit(solution)/shard_map/reduce_sum | solution.py:27
  162.9 35.3 %psum.7 = f32[4096]{0:T(1024)S(1)} all-reduce(f32[4096]{0:T(1024)S(1)} %fusion), channel_id=1, replica_groups=mesh['dp'=4,'seq'=4,'tensor'=2] {'seq','tensor'}, use_global_device_ids=true, to_apply=%region_11.13 | all-reduce | flops 4096 | bytes 32768 | tf_op jit(solution)/shard_map/psum | solution.py:104
  198.2 0.0 copy-done.4
  198.2 10.2 %fusion.2 = bf16[4096,1024]{1,0:T(8,128)(2,1)} fusion(f32[1024]{0:T(1024)S(1)} %copy-done.4, f32[4096]{0:T(1024)S(1)} %add_rsqrt_fusion, bf16[4096,1024]{1,0:T(8,128)(2,1)} %param.16, bf16[32,128,1024]{2,1,0:T(8,128)(2,1)} %gather_fusion.1, pred[4096]{0:T(1024)(128)(4,1)S(1)} %broadcast_bitcast_fusion), kind=kLoop, calls=%fused_computation.8 | loop fusion | flops 20971520 | bytes 25190400 | tf_op jit(solution)/shard_map/convert_element_type | solution.py:106
  (20 shorter events, 0.2 us)
Async XLA Ops:
  0.0 102.2 %copy-start = (s32[4,32]{1,0:T(4,128)S(1)}, s32[4,32]{1,0:T(4,128)}, u32[]{:S(2)}) copy-start(s32[4,32]{1,0:T(4,128)} %param.19) | copy-start | bytes 1540
  0.0 18.2 %copy-start.2 = (f32[4,1024]{1,0:T(4,128)S(1)}, f32[4,1024]{1,0:T(4,128)}, u32[]{:S(2)}) copy-start(f32[4,1024]{1,0:T(4,128)} %param.15) | copy-start | bytes 49156
  0.0 18.2 %copy-start.1 = (bf16[256,3200]{1,0:T(8,128)(2,1)S(1)}, bf16[256,3200]{1,0:T(8,128)(2,1)}, u32[]{:S(2)}) copy-start(bf16[256,3200]{1,0:T(8,128)(2,1)} %param.11) | copy-start | bytes 4915204
  0.0 19.1 %copy-start.5 = (f32[3200]{0:T(1024)S(1)}, f32[3200]{0:T(1024)}, u32[]{:S(2)}) copy-start(f32[3200]{0:T(1024)} %param.13) | copy-start | bytes 38404
  0.0 19.2 %copy-start.6 = (f32[3200]{0:T(1024)S(1)}, f32[3200]{0:T(1024)}, u32[]{:S(2)}) copy-start(f32[3200]{0:T(1024)} %param.12) | copy-start | bytes 38404
  31.5 7.9 %copy-start.3 = (s32[32,1]{0,1:T(1,128)S(1)}, s32[32,1]{0,1:T(1,128)}, u32[]{:S(2)}) copy-start(s32[32,1]{0,1:T(1,128)} %param.18) | copy-start | bytes 388
  33.0 54.6 %all-to-all-start = ((bf16[256,4,1024]{2,0,1:T(8,128)(2,1)}), bf16[256,4,1024]{2,0,1:T(8,128)(2,1)S(1)}, u32[]{:S(2)}, u32[]{:S(2)}) async-start(bf16[256,4,1024]{2,0,1:T(8,128)(2,1)} %bitcast.43), calls=%async_computation | async-start | bytes 4194304 | tf_op jit(solution)/shard_map/all_to_all | solution.py:49
  95.0 53.1 %all-to-all-start.1 = ((bf16[4,4,128,1024]{3,2,1,0:T(8,128)(2,1)}), bf16[4,4,128,1024]{3,2,1,0:T(8,128)(2,1)}, u32[]{:S(2)}, u32[]{:S(2)}) async-start(bf16[4,4,128,1024]{3,2,1,0:T(8,128)(2,1)} %broadcast_select_fusion), calls=%async_computation.1 | async-start | bytes 8388608 | tf_op jit(solution)/shard_map/all_to_all | solution.py:91
  155.2 43.0 %copy-start.4 = (f32[1024]{0:T(1024)S(1)}, f32[1024]{0:T(1024)}, u32[]{:S(2)}) copy-start(f32[1024]{0:T(1024)} %param.17) | copy-start | bytes 12292
where the time goes:
time: 209 us; the launch traced here: 208 us
  waiting for transfers between devices  91.6 us (44%)
  blocking collectives  35.3 us (17%)
  local copies, waits for them, and re-layouts  32.1 us (15%)
  other arithmetic  25.8 us (12%)
  matrix products  12.3 us (6%)
  starting transfers between devices  11.3 us (5%)
    all_to_all x1, waiting for transfers between devices, local(): lax.all_to_all(projected.reshape(local_rows, owners, column_block), 'seq'...  47.6 us
    all_to_all x1, waiting for transfers between devices, local(): lax.all_to_all(outgoing, 'dp', split_axis=0, concat_axis=0, tiled=True)  43.9 us
    psum x1, blocking collectives, local(): totals = lax.psum(squares, ('seq', 'tensor'))  35.3 us
    unnamed x17, local copies, waits for them, and re-layouts  18.8 us
    dot_general x1, matrix products, local(): jnp.dot(normed_in, weights_flat, preferred_element_type=jnp.float32)  12.3 us
    convert_element_type x1, other arithmetic, local(): (assembled.astype(jnp.float32) * scale[:, None] * norm_gain).astype(jnp.b...  10.2 us
    reduce_sum x1, other arithmetic, row_squares(): return jnp.sum(values * values, axis=-1)  7.74 us
    gather x1, local copies, waits for them, and re-layouts, local(): picked = incoming[jnp.clip(arrival_index, 0, replicas * capacity - 1)]  7.09 us
  transfers between devices with their start and end apart: 2, of which 2 were waited for; matrix products, arithmetic and copies ran while one was open for 2% of the time, Pallas kernels for 0%

commit v1 on v0

v1 whole, which is shorter than its diff:
```python
import functools

import jax
import jax.numpy as jnp
from jax import lax
from jax.experimental import pallas as pl
from jax.experimental.pallas import tpu as pltpu
from jax.sharding import PartitionSpec as P

TILE = 128
CORES = 2
STAT_ROWS = 8
MESH = pl.DeviceIdType.MESH


def layer_norm(rows, ln_gain, ln_bias):
    values = rows.astype(jnp.float32)
    center = values - jnp.mean(values, axis=-1, keepdims=True)
    spread = jnp.mean(center * center, axis=-1, keepdims=True)
    return (center * lax.rsqrt(spread + 1e-06) * ln_gain + ln_bias).astype(jnp.bfloat16)


def send_order(place, owners):
    toward = 1 if place < owners // 2 else -1
    steps = [0, 1] + list(range(2, owners))
    return [(place + toward * step) % owners for step in steps]


def arrival_order(place, owners):
    return sorted(range(owners), key=lambda other: (abs(other - place), -abs(2 * other - owners + 1)))


def lookup(index, table):
    value = jnp.int32(table[0])
    for entry in range(1, len(table)):
        value = jnp.where(index == entry, jnp.int32(table[entry]), value)
    return value


def exchange_kernel(
    sizes,
    proj_ref,
    stat_ref,
    out_ref,
    text_ref,
    vision_ref,
    y_land,
    z_land,
    d_land,
    local_sem,
    zs_sem,
    zr_sem,
    xs_sem,
    xr_sem,
    cs_sem,
    cr_sem,
    ys_sem,
    yr_sem,
    zss_sem,
    zsr_sem,
    ds_sem,
    dr_sem,
):
    replicas, owners, splits, tiles = sizes
    chips = replicas // CORES
    mine = lax.axis_index("dp")
    place = lax.axis_index("seq")
    half = lax.axis_index("tensor")
    chip = mine // CORES
    core = mine % CORES
    partner = chip * CORES + 1 - core

    barrier = pltpu.get_barrier_semaphore()
    for step in range(1, replicas):
        pl.semaphore_signal(
            barrier, inc=1, device_id={"dp": (mine + step) % replicas}, device_id_type=MESH
        )
    for step in range(1, owners):
        pl.semaphore_signal(
            barrier, inc=1, device_id={"seq": (place + step) % owners}, device_id_type=MESH
        )
    for step in range(1, splits):
        pl.semaphore_signal(
            barrier, inc=1, device_id={"tensor": (half + step) % splits}, device_id_type=MESH
        )
    pl.semaphore_wait(barrier, replicas + owners + splits - 3)

    sends = []

    def push(src, dst, send_sem, recv_sem, device):
        copy = pltpu.make_async_remote_copy(
            src_ref=src,
            dst_ref=dst,
            send_sem=send_sem,
            recv_sem=recv_sem,
            device_id=device,
            device_id_type=MESH,
        )
        copy.start()
        sends.append(copy)

    def arrived(dst, send_sem, recv_sem, device):
        pltpu.make_async_remote_copy(
            src_ref=dst,
            dst_ref=dst,
            send_sem=send_sem,
            recv_sem=recv_sem,
            device_id=device,
            device_id_type=MESH,
        ).wait_recv()

    y_sends = []
    for step in range(1, splits):
        other = (half + step) % splits
        push(
            stat_ref,
            y_land.at[half],
            ys_sem.at[step],
            yr_sem.at[half],
            {"tensor": other},
        )

    targets = [
        lookup(place, [send_order(p, owners)[k] for p in range(owners)]) for k in range(owners)
    ]
    sources = [
        lookup(place, [arrival_order(p, owners)[k] for p in range(owners)]) for k in range(owners)
    ]

    for k in range(1, owners):
        for tile in range(tiles):
            push(
                proj_ref.at[targets[k], tile],
                out_ref.at[mine, place, tile],
                zs_sem.at[k, tile],
                zr_sem.at[place, tile],
                {"seq": targets[k]},
            )

    def spread(src, k, tile):
        owner = sources[k]
        for step in range(1, chips):
            other = (chip + step) % chips
            push(
                src,
                out_ref.at[mine, owner, tile],
                xs_sem.at[step, k, tile],
                xr_sem.at[chip, owner, tile],
                {"dp": other * CORES + core},
            )
        push(
            src,
            out_ref.at[mine, owner, tile],
            cs_sem.at[0, k, tile],
            cr_sem.at[chip, owner, tile],
            {"dp": partner},
        )

    def relay(k, tile):
        owner = sources[k]
        for step in range(1, chips):
            other = (chip + chips - step) % chips
            origin = other * CORES + core
            block = out_ref.at[origin, owner, tile]
            arrived(block, xs_sem.at[step, k, tile], xr_sem.at[other, owner, tile], {"dp": origin})
            push(
                block,
                block,
                cs_sem.at[step, k, tile],
                cr_sem.at[other, owner, tile],
                {"dp": partner},
            )

    for tile in range(tiles):
        spread(proj_ref.at[place, tile], 0, tile)
    keep = pltpu.make_async_copy(proj_ref.at[place], out_ref.at[mine, place], local_sem)
    keep.start()

    total = stat_ref[...]
    for step in range(1, splits):
        other = (half + step) % splits
        arrived(y_land.at[other], ys_sem.at[step], yr_sem.at[other], {"tensor": other})
        total = total + y_land[other]
    z_land[place] = total
    for step in range(1, owners):
        other = (place + step) % owners
        push(
            z_land.at[place],
            z_land.at[place],
            zss_sem.at[step],
            zsr_sem.at[place],
            {"seq": other},
        )

    def statistics():
        text_total = jnp.zeros(text_ref.shape, jnp.float32)
        for step in range(1, owners):
            other = (place + step) % owners
            arrived(z_land.at[other], zss_sem.at[step], zsr_sem.at[other], {"seq": other})
        for owner in range(owners):
            text_total = text_total + z_land[owner, STAT_ROWS:, :]
            d_land[mine, owner] = z_land[owner, :STAT_ROWS, :]
        text_ref[...] = text_total
        for step in range(1, replicas):
            other = (mine + step) % replicas
            push(
                d_land.at[mine],
                d_land.at[mine],
                ds_sem.at[step],
                dr_sem.at[mine],
                {"dp": other},
            )

    for k in range(1, owners):
        for tile in range(tiles):
            arrived(
                out_ref.at[mine, sources[k], tile],
                zs_sem.at[k, tile],
                zr_sem.at[sources[k], tile],
                {"seq": sources[k]},
            )
            spread(out_ref.at[mine, sources[k], tile], k, tile)
        if k == owners - 1:
            statistics()
        for tile in range(tiles):
            relay(k - 1, tile)
    for tile in range(tiles):
        relay(owners - 1, tile)

    for step in range(1, replicas):
        other = (mine + step) % replicas
        arrived(d_land.at[other], ds_sem.at[step], dr_sem.at[other], {"dp": other})
    vision_ref[...] = d_land[...]
    for k in range(owners):
        for other in range(chips):
            origin = other * CORES + 1 - core
            for tile in range(tiles):
                arrived(
                    out_ref.at[origin, sources[k], tile],
                    cs_sem.at[0, k, tile],
                    cr_sem.at[other, sources[k], tile],
                    {"dp": partner},
                )
    keep.wait()
    for copy in sends:
        copy.wait_send()


def exchange(blocks, stats, sizes):
    replicas, owners, splits, tiles = sizes
    chips = replicas // CORES
    columns = blocks.shape[-1]
    rows = stats.shape[0]
    dma = pltpu.SemaphoreType.DMA
    return pl.pallas_call(
        functools.partial(exchange_kernel, sizes),
        out_shape=(
            jax.ShapeDtypeStruct((replicas, owners, tiles, TILE, columns), jnp.bfloat16),
            jax.ShapeDtypeStruct((rows - STAT_ROWS, TILE), jnp.float32),
            jax.ShapeDtypeStruct((replicas, owners, STAT_ROWS, TILE), jnp.float32),
        ),
        in_specs=[pl.BlockSpec(memory_space=pltpu.VMEM)] * 2,
        out_specs=(
            pl.BlockSpec(memory_space=pl.ANY),
            pl.BlockSpec(memory_space=pltpu.VMEM),
            pl.BlockSpec(memory_space=pltpu.VMEM),
        ),
        scratch_shapes=[
            pltpu.VMEM((splits, rows, TILE), jnp.float32),
            pltpu.VMEM((owners, rows, TILE), jnp.float32),
            pltpu.VMEM((replicas, owners, STAT_ROWS, TILE), jnp.float32),
            dma,
            dma((owners, tiles)),
            dma((owners, tiles)),
            dma((chips, owners, tiles)),
            dma((chips, owners, tiles)),
            dma((chips, owners, tiles)),
            dma((chips, owners, tiles)),
            dma((splits,)),
            dma((splits,)),
            dma((owners,)),
            dma((owners,)),
            dma((replicas,)),
            dma((replicas,)),
        ],
        compiler_params=pltpu.CompilerParams(collective_id=0, has_side_effects=True),
        name="exchange",
    )(blocks, stats)


def place_kernel(group, width, source_ref, *refs):
    picked = refs[:group]
    text_ref, text_sum, vision_sum, gain_ref, out_ref = refs[group:]
    first = pl.program_id(0) * group
    gain = gain_ref[...]
    for item in range(group):
        source = source_ref[first + item]
        rows = slice(item * TILE, (item + 1) * TILE)

        def scaled(values, squares):
            scale = lax.rsqrt(squares / width + 1e-05)
            column = jnp.broadcast_to(scale, (TILE, TILE)).T
            for start in range(0, out_ref.shape[1], TILE):
                lanes = slice(start, start + TILE)
                out_ref[rows, lanes] = (
                    values[:, lanes].astype(jnp.float32) * column * gain[:, lanes]
                ).astype(jnp.bfloat16)

        @pl.when(source >= 0)
        def _():
            scaled(picked[item][0], vision_sum[pl.ds(source, 1), :])

        @pl.when(source < 0)
        def _():
            scaled(text_ref[rows, :], text_sum[pl.ds(first + item, 1), :])


def place(source_tile, gathered, text_embed, text_sum, vision_sum, norm_gain, width):
    positions = source_tile.shape[0]
    group = 4
    columns = text_embed.shape[1]

    def pick(item):
        return lambda step, source: (jnp.maximum(source[step * group + item], 0), 0, 0)

    whole = lambda step, source: (0, 0)
    return pl.pallas_call(
        functools.partial(place_kernel, group, width),
        grid_spec=pltpu.PrefetchScalarGridSpec(
            num_scalar_prefetch=1,
            grid=(positions // group,),
            in_specs=[pl.BlockSpec((1, TILE, columns), pick(item)) for item in range(group)]
            + [
                pl.BlockSpec((group * TILE, columns), lambda step, source: (step, 0)),
                pl.BlockSpec(text_sum.shape, whole),
                pl.BlockSpec(vision_sum.shape, whole),
                pl.BlockSpec((1, columns), whole),
            ],
            out_specs=pl.BlockSpec((group * TILE, columns), lambda step, source: (step, 0)),
        ),
        out_shape=jax.ShapeDtypeStruct(text_embed.shape, jnp.bfloat16),
        name="place",
    )(source_tile, *([gathered] * group), text_embed, text_sum, vision_sum, norm_gain[None, :])


def local(
    vit_out, ln_gain, ln_bias, proj_weight, proj_bias, text_embed, norm_gain, tile_dest, tile_place
):
    replicas = lax.axis_size("dp")
    owners = lax.axis_size("seq")
    splits = lax.axis_size("tensor")
    mine = lax.axis_index("dp")
    local_rows = vit_out.shape[0]
    width_in = vit_out.shape[1]
    columns = proj_weight.shape[2]
    positions = tile_place.shape[1]
    total_tiles = tile_dest.shape[0]
    tiles = local_rows // TILE
    sizes = (replicas, owners, splits, tiles)

    normed_in = layer_norm(vit_out, ln_gain, ln_bias)
    hidden = jnp.dot(
        normed_in,
        proj_weight.reshape(width_in, owners * columns),
        preferred_element_type=jnp.float32,
    ) + proj_bias.reshape(-1)
    projected = hidden.astype(jnp.bfloat16)
    own_squares = jnp.sum(jnp.square(projected.astype(jnp.float32)), axis=-1)
    text_squares = jnp.sum(jnp.square(text_embed.astype(jnp.float32)), axis=-1)
    stats = jnp.concatenate(
        [
            jnp.pad(own_squares.reshape(tiles, TILE), ((0, STAT_ROWS - tiles), (0, 0))),
            text_squares.reshape(positions, TILE),
        ]
    )
    blocks = projected.reshape(tiles, TILE, owners, columns).transpose(2, 0, 1, 3)
    gathered, text_sum, vision_sum = exchange(blocks, stats, sizes)

    named = tile_dest[:, 0] == mine
    earlier = jnp.arange(total_tiles)[None, :] < jnp.arange(total_tiles)[:, None]
    ranks = jnp.sum((earlier & named[None, :]).astype(jnp.int32), axis=1)
    place_row = lax.dynamic_index_in_dim(tile_place, mine, 0, keepdims=False)
    numbers = jnp.arange(positions, dtype=jnp.int32)
    order = jnp.sum(
        jnp.where(place_row[None, :] == numbers[:, None], numbers[None, :], 0), axis=1
    )
    matches = named[None, :] & (ranks[None, :] == order[:, None])
    source_tile = jnp.max(
        jnp.where(matches, jnp.arange(total_tiles, dtype=jnp.int32)[None, :], -1), axis=1
    )
    return place(
        source_tile,
        gathered.reshape(total_tiles, TILE, columns),
        text_embed,
        text_sum,
        vision_sum[:, :, :tiles, :].reshape(total_tiles, TILE),
        norm_gain,
        norm_gain.shape[0] * owners * splits,
    )


def solution(mesh):
    placed = (
        P(("dp", "seq"), None),
        P(),
        P(),
        P(None, None, "tensor"),
        P(None, "tensor"),
        P("dp", ("seq", "tensor")),
        P(("seq", "tensor")),
        P(),
        P(),
    )
    return jax.shard_map(
        local, mesh=mesh, in_specs=placed, out_specs=P("dp", ("seq", "tensor")), check_vma=False
    )
```

time: 209 us -> 139 us (0.67)
  waiting for transfers between devices: 91.6 us -> 0 us
  Pallas kernels: 0 us -> 88.7 us
  blocking collectives: 35.3 us -> 0 us
  other arithmetic: 25.8 us -> 11 us
  starting transfers between devices: 11.3 us -> 0 us
  local copies, waits for them, and re-layouts: 32.1 us -> 25.6 us
    all_to_all x2 -> x0, waiting for transfers between devices: 91.6 us -> none  [the longest x1 47.6 us: local(): lax.all_to_all(projected.reshape(local_rows, owners, column_block), 'seq'...]
    pallas_call x0 -> x2, Pallas kernels: none -> 88.7 us  [the longest x1 75.4 us: exchange(): pl.pallas_call(functools.partial(exchange_kernel, sizes), out_shape=(jax....]
    psum x1 -> x0, blocking collectives: 35.3 us -> none  [local(): totals = lax.psum(squares, ('seq', 'tensor'))]
    gather x4 -> x0, local copies, waits for them, and re-layouts: 11.3 us -> none  [the longest x1 7.09 us: local(): picked = incoming[jnp.clip(arrival_index, 0, replicas * capacity - 1)]]
    all_to_all x2 -> x0, starting transfers between devices: 11.3 us -> none  [the longest x1 6.37 us: local(): lax.all_to_all(projected.reshape(local_rows, owners, column_block), 'seq'...]
    convert_element_type x4 -> x0, other arithmetic: 10.3 us -> none  [the longest x1 10.2 us: local(): (assembled.astype(jnp.float32) * scale[:, None] * norm_gain).astype(jnp.b...]
    select_n x6 -> x0, other arithmetic: 4.59 us -> none  [the longest x1 4.54 us: local(): jnp.where((slot_source >= 0)[:, None, None], tiles[jnp.clip(slot_source,...]
    reshape x2, local copies, waits for them, and re-layouts: 1.58 us -> 5.27 us  [local(): projected.reshape(tiles, TILE, owners, columns).transpose(2, 0, 1, 3)]
  transfers between devices with their start and end apart: 2 -> 0, of which waited for: 2 -> 0; matrix products, arithmetic and copies ran while one was open for 2% -> 0% of each run, Pallas kernels for 0% -> 0%
where the time goes in v1:
time: 139 us
  Pallas kernels  88.7 us (64%)
  local copies, waits for them, and re-layouts  25.6 us (18%)
  matrix products  13.6 us (10%)
  other arithmetic  11 us (8%)
    pallas_call x1, Pallas kernels, exchange(): pl.pallas_call(functools.partial(exchange_kernel, sizes), out_shape=(jax....  75.4 us
    unnamed x14, local copies, waits for them, and re-layouts  18.9 us
    dot_general x1, matrix products, local(): jnp.dot(normed_in, proj_weight.reshape(width_in, owners * columns), prefe...  13.6 us
    pallas_call x1, Pallas kernels, place(): pl.pallas_call(functools.partial(place_kernel, group, width), grid_spec=p...  13.3 us
    reshape x2, local copies, waits for them, and re-layouts, local(): projected.reshape(tiles, TILE, owners, columns).transpose(2, 0, 1, 3)  5.27 us
    reduce_sum x1, other arithmetic, local(): text_squares = jnp.sum(jnp.square(text_embed.astype(jnp.float32)), axis=-1)  5.09 us

profile of v1, /device:TPU:0, one launch (start us, length us, event | category | flops | bytes accessed | tf_op | source)
XLA Modules:
  0.0 139.0 jit_solution(14945475275088004373)
XLA Ops:
  0.0 0.0 copy-start
  0.0 0.7 copy-done
  0.7 0.7 compare_bitcast_fusion
  1.3 0.1 select_reduce_fusion.1
  1.5 0.8 select_reduce_fusion.source_ref
  2.2 1.7 %convert_reduce_fusion = f32[256]{0:T(256)S(1)} fusion(bf16[256,3200]{1,0:T(8,128)(2,1)} %param.9), kind=kLoop, calls=%fused_computation.5 | loop fusion | flops 1638144 | bytes 1639424 | tf_op jit(solution)/shard_map/reduce_sum | solution.py:18
  4.0 2.0 %fusion.3 = f32[256]{0:T(256)S(1)} fusion(bf16[256,3200]{1,0:T(8,128)(2,1)} %param.9, f32[256]{0:T(256)S(1)} %broadcast_multiply_fusion), kind=kLoop, calls=%fused_computation.8 | loop fusion | flops 3276544 | bytes 1640448 | tf_op jit(solution)/shard_map/reduce_sum | solution.py:19
  6.0 0.0 copy-start.3
  6.0 0.0 copy-start.2
  6.0 0.0 copy-start.4
  6.0 0.0 copy-start.5
  6.0 18.2 %copy.12 = bf16[400,8,4,1024]{3,1,2,0:T(8,128)(2,1)} copy(bf16[400,8,4,1024]{3,2,1,0:T(4,128)(2,1)} %bitcast.23) | data formatting | bytes 52428800
  24.2 0.0 copy-done.3
  24.3 0.0 copy-done.2
  24.3 0.0 copy-done.4
  24.3 0.0 copy-done.5
  24.3 13.6 %multiply_reduce_fusion.1 = (f32[256]{0:T(256)S(1)}, bf16[256,4096]{1,0:T(8,128)(2,1)}) fusion(f32[4096]{0:T(1024)S(1)} %bitcast.29, bf16[3200,4096]{1,0:T(8,128)(2,1)} %bitcast.24, bf16[256,3200]{1,0:T(8,128)(2,1)S(1)} %copy-done.2, f32[3200]{0:T(1024)S(1)} %copy-done.4, f32[3200]{0:T(1024)S(1)} %copy-done.5, f32[256]{0:T(256)S(1)} %add_rsqrt_fusion, ...), kind=kOutput, calls=%fused_computation.3 | convolution fusion | flops 6721044480 | bytes 29995008 | tf_op jit(solution)/shard_map/dot_general | solution.py:362
  37.8 3.3 %reshape.43 = bf16[2,128,4,1024]{3,2,1,0:T(4,128)(2,1)S(1)} reshape(bf16[256,4096]{1,0:T(8,128)(2,1)} %get-tuple-element.12) | data formatting | bytes 4194304 | tf_op jit(solution)/shard_map/reshape | solution.py:376
  41.2 1.9 %copy.16 = bf16[2,128,4,1024]{3,1,0,2:T(8,128)(2,1)} copy(bf16[2,128,4,1024]{3,2,1,0:T(4,128)(2,1)S(1)} %reshape.43) | data formatting | bytes 4194304 | tf_op jit(solution)/shard_map/reshape | solution.py:376
  43.1 5.1 %multiply_reduce_fusion = f32[4096]{0:T(1024)S(1)} fusion(bf16[4096,1024]{1,0:T(8,128)(2,1)} %refs_4_.1), kind=kLoop, calls=%fused_computation | loop fusion | flops 12578816 | bytes 8404992 | tf_op jit(solution)/shard_map/reduce_sum | solution.py:369
  48.2 0.6 select_maximum_fusion.stat_ref
  48.8 75.4 %exchange.1 = (bf16[4,4,2,128,1024]{4,3,2,1,0:T(8,128)(2,1)}, f32[32,128]{1,0:T(8,128)}, f32[4,4,8,128]{3,2,1,0:T(8,128)}) custom-call(bf16[4,2,128,1024]{3,2,1,0:T(8,128)(2,1)} %bitcast.25, f32[40,128]{1,0:T(8,128)} %select_maximum_fusion.stat_ref), custom_call_target="tpu_custom_call" | custom-call | tf_op jit(solution)/shard_map/exchange/pallas_call | solution.py:255
  124.3 1.4 %slice.3 = f32[4,4,2,128]{3,2,1,0:T(2,128)} slice(f32[4,4,8,128]{3,2,1,0:T(8,128)} %get-tuple-element.10), slice={[0:4], [0:4], [0:2], [0:128]} | slice | bytes 32768 | tf_op jit(solution)/shard_map/slice | solution.py:396
  125.7 0.0 copy-start.1
  125.7 13.3 %place.1 = bf16[4096,1024]{1,0:T(8,128)(2,1)} custom-call(s32[32]{0:T(128)} %select_reduce_fusion.source_ref, bf16[32,128,1024]{2,1,0:T(8,128)(2,1)} %bitcast.19, bf16[32,128,1024]{2,1,0:T(8,128)(2,1)} %bitcast.20, bf16[32,128,1024]{2,1,0:T(8,128)(2,1)} %bitcast.21, bf16[32,128,1024]{2,1,0:T(8,128)(2,1)} %bitcast.22, bf16[4096,1024]{1,0:T(8,128)(2,1)} %refs_4_.1, ...), custom_call_target="tpu_custom_call" | custom-call | tf_op jit(solution)/shard_map/place/pallas_call | solution.py:327
  139.0 0.0 copy-done.1
  (4 shorter events, 0.0 us)
Async XLA Ops:
  0.0 0.7 copy-start
  6.0 18.3 %copy-start.3 = (f32[4,1024]{1,0:T(4,128)S(1)}, f32[4,1024]{1,0:T(4,128)}, u32[]{:S(2)}) copy-start(f32[4,1024]{1,0:T(4,128)} %param.13) | copy-start | bytes 49156
  6.0 18.3 %copy-start.2 = (bf16[256,3200]{1,0:T(8,128)(2,1)S(1)}, bf16[256,3200]{1,0:T(8,128)(2,1)}, u32[]{:S(2)}) copy-start(bf16[256,3200]{1,0:T(8,128)(2,1)} %param.9) | copy-start | bytes 4915204
  6.0 18.3 %copy-start.4 = (f32[3200]{0:T(1024)S(1)}, f32[3200]{0:T(1024)}, u32[]{:S(2)}) copy-start(f32[3200]{0:T(1024)} %param.11) | copy-start | bytes 38404
  6.0 18.3 %copy-start.5 = (f32[3200]{0:T(1024)S(1)}, f32[3200]{0:T(1024)}, u32[]{:S(2)}) copy-start(f32[3200]{0:T(1024)} %param.10) | copy-start | bytes 38404
  125.7 13.3 %copy-start.1 = (s32[4,32]{1,0:T(4,128)S(1)}, s32[4,32]{1,0:T(4,128)}, u32[]{:S(2)}) copy-start(s32[4,32]{1,0:T(4,128)} %param.17) | copy-start | bytes 1540

commit v2 on v1

--- a/solution.py
+++ b/solution.py
@@ -10,6 +10,7 @@
 TILE = 128
 CORES = 2
 STAT_ROWS = 8
+DEPTH = 640
 MESH = pl.DeviceIdType.MESH
 
 
@@ -288,6 +289,99 @@
     )(blocks, stats)
 
 
+def tile_squares(values, rows):
+    columns = values.shape[1]
+    part = jnp.zeros((rows, TILE), jnp.float32)
+    for start in range(0, columns, TILE):
+        lanes = values[:, start : start + TILE].astype(jnp.float32)
+        part = part + lanes * lanes
+    return part
+
+
+def project_kernel(
+    depth,
+    text_steps,
+    rows_ref,
+    weight_ref,
+    bias_ref,
+    text_ref,
+    block_ref,
+    own_ref,
+    text_out,
+    total,
+):
+    step = pl.program_id(0)
+    owners, tiles, _, columns = block_ref.shape
+
+    @pl.when(step == 0)
+    def _():
+        own_ref[...] = jnp.zeros_like(own_ref)
+
+    for owner in range(owners):
+        term = jnp.dot(
+            rows_ref[...], weight_ref[:, owner * columns : (owner + 1) * columns], preferred_element_type=jnp.float32
+        )
+
+        @pl.when(step == 0)
+        def _():
+            total[owner] = term + bias_ref[pl.ds(owner, 1), :]
+
+        @pl.when(step > 0)
+        def _():
+            total[owner] += term
+
+    @pl.when(step < text_steps)
+    def _():
+        for item in range(text_out.shape[0]):
+            part = tile_squares(text_ref[item * TILE : (item + 1) * TILE, :], TILE)
+            text_out[item] = jnp.sum(part.T, axis=0, keepdims=True)
+
+    @pl.when(step == depth - 1)
+    def _():
+        for tile in range(tiles):
+            part = jnp.zeros((TILE, TILE), jnp.float32)
+            for owner in range(owners):
+                values = total[owner, tile * TILE : (tile + 1) * TILE, :].astype(jnp.bfloat16)
+                block_ref[owner, tile] = values
+                part = part + tile_squares(values, TILE)
+            own_ref[tile : tile + 1, :] = jnp.sum(part.T, axis=0, keepdims=True)
+
+
+def project(rows, weight, bias, text_embed, positions):
+    count, width = rows.shape
+    owners, columns = weight.shape[1:]
+    flat = weight.reshape(width, owners * columns)
+    tiles = count // TILE
+    cut = max(c for c in range(TILE, DEPTH + 1, TILE) if width % c == 0)
+    depth = width // cut
+    text_steps = max(c for c in range(1, depth + 1) if positions % c == 0)
+    group = positions // text_steps
+    last = text_steps - 1
+    return pl.pallas_call(
+        functools.partial(project_kernel, depth, text_steps),
+        grid=(depth,),
+        in_specs=[
+            pl.BlockSpec((count, cut), lambda step: (0, step)),
+            pl.BlockSpec((cut, owners * columns), lambda step: (step, 0)),
+            pl.BlockSpec(bias.shape, lambda step: (0, 0)),
+            pl.BlockSpec((group * TILE, columns), lambda step: (jnp.minimum(step, last), 0)),
+        ],
+        out_specs=(
+            pl.BlockSpec((owners, tiles, TILE, columns), lambda step: (0, 0, 0, 0)),
+            pl.BlockSpec((STAT_ROWS, TILE), lambda step: (0, 0)),
+            pl.BlockSpec((group, 1, TILE), lambda step: (jnp.minimum(step, last), 0, 0)),
+        ),
+        out_shape=(
+            jax.ShapeDtypeStruct((owners, tiles, TILE, columns), jnp.bfloat16),
+            jax.ShapeDtypeStruct((STAT_ROWS, TILE), jnp.float32),
+            jax.ShapeDtypeStruct((positions, 1, TILE), jnp.float32),
+        ),
+        scratch_shapes=[pltpu.VMEM((owners, count, columns), jnp.float32)],
+        compiler_params=pltpu.CompilerParams(vmem_limit_bytes=50 * 2**20),
+        name="project",
+    )(rows, flat, bias, text_embed)
+
+
 def place_kernel(group, width, source_ref, *refs):
     picked = refs[:group]
     text_ref, text_sum, vision_sum, gain_ref, out_ref = refs[group:]
@@ -351,7 +445,6 @@
     splits = lax.axis_size("tensor")
     mine = lax.axis_index("dp")
     local_rows = vit_out.shape[0]
-    width_in = vit_out.shape[1]
     columns = proj_weight.shape[2]
     positions = tile_place.shape[1]
     total_tiles = tile_dest.shape[0]
@@ -359,21 +452,10 @@
     sizes = (replicas, owners, splits, tiles)
 
     normed_in = layer_norm(vit_out, ln_gain, ln_bias)
-    hidden = jnp.dot(
-        normed_in,
-        proj_weight.reshape(width_in, owners * columns),
-        preferred_element_type=jnp.float32,
-    ) + proj_bias.reshape(-1)
-    projected = hidden.astype(jnp.bfloat16)
-    own_squares = jnp.sum(jnp.square(projected.astype(jnp.float32)), axis=-1)
-    text_squares = jnp.sum(jnp.square(text_embed.astype(jnp.float32)), axis=-1)
-    stats = jnp.concatenate(
-        [
-            jnp.pad(own_squares.reshape(tiles, TILE), ((0, STAT_ROWS - tiles), (0, 0))),
-            text_squares.reshape(positions, TILE),
-        ]
-    )
-    blocks = projected.reshape(tiles, TILE, owners, columns).transpose(2, 0, 1, 3)
+    blocks, own_squares, text_squares = project(
+        normed_in, proj_weight, proj_bias, text_embed, positions
+    )
+    stats = jnp.concatenate([own_squares, text_squares.reshape(positions, TILE)])
     gathered, text_sum, vision_sum = exchange(blocks, stats, sizes)
 
     named = tile_dest[:, 0] == mine

time: 139 us -> 136 us (0.978)
  Pallas kernels: 88.7 us -> 107 us
  matrix products: 13.6 us -> 0 us
  other arithmetic: 11 us -> 6.73 us
  local copies, waits for them, and re-layouts: 25.6 us -> 21.5 us
    pallas_call x0 -> x1, Pallas kernels: none -> 19.2 us  [project(): pl.pallas_call(functools.partial(project_kernel, depth, text_steps), grid...]
    dot_general x1 -> x0, matrix products: 13.6 us -> none  [local(): jnp.dot(normed_in, proj_weight.reshape(width_in, owners * columns), prefe...]
    reshape x2 -> x0, local copies, waits for them, and re-layouts: 5.27 us -> none  [local(): projected.reshape(tiles, TILE, owners, columns).transpose(2, 0, 1, 3)]
    reduce_sum x1 -> x0, other arithmetic: 5.09 us -> none  [local(): text_squares = jnp.sum(jnp.square(text_embed.astype(jnp.float32)), axis=-1)]
    unnamed x14 -> x15, local copies, waits for them, and re-layouts: 18.9 us -> 20.1 us
where the time goes in v2:
time: 136 us
  Pallas kernels  107 us (79%)
  local copies, waits for them, and re-layouts  21.5 us (16%)
  other arithmetic  6.73 us (5%)
    pallas_call x1, Pallas kernels, exchange(): pl.pallas_call(functools.partial(exchange_kernel, sizes), out_shape=(jax....  75.5 us
    unnamed x15, local copies, waits for them, and re-layouts  20.1 us
    pallas_call x1, Pallas kernels, project(): pl.pallas_call(functools.partial(project_kernel, depth, text_steps), grid...  19.2 us
    pallas_call x1, Pallas kernels, place(): pl.pallas_call(functools.partial(place_kernel, group, width), grid_spec=p...  12.7 us

profile of v2, /device:TPU:0, one launch (start us, length us, event | category | flops | bytes accessed | tf_op | source)
XLA Modules:
  0.0 135.8 jit_solution(9655406483577966279)
XLA Ops:
  0.0 0.0 copy-start
  0.0 0.0 copy-start.4
  0.0 0.0 copy-start.5
  0.0 0.0 copy-start.6
  0.0 0.7 copy-done
  0.7 0.7 compare_bitcast_fusion
  1.3 0.1 select_reduce_fusion.1
  1.5 0.8 select_reduce_fusion.source_ref
  2.2 1.7 %convert_reduce_fusion = f32[256]{0:T(256)S(1)} fusion(bf16[256,3200]{1,0:T(8,128)(2,1)} %param.9), kind=kLoop, calls=%fused_computation.1 | loop fusion | flops 1638144 | bytes 1639424 | tf_op jit(solution)/shard_map/reduce_sum | solution.py:19
  4.0 2.0 %fusion.2 = f32[256]{0:T(256)S(1)} fusion(bf16[256,3200]{1,0:T(8,128)(2,1)} %param.9, f32[256]{0:T(256)S(1)} %broadcast_multiply_fusion), kind=kLoop, calls=%fused_computation.4 | loop fusion | flops 3276544 | bytes 1640448 | tf_op jit(solution)/shard_map/reduce_sum | solution.py:20
  6.0 0.0 copy-done.4
  6.0 0.0 copy-done.5
  6.0 0.0 copy-done.6
  6.0 0.8 fusion.5.rows_ref
  6.9 0.0 copy-start.3
  6.9 18.1 %copy.10 = bf16[400,8,4,1024]{3,1,2,0:T(8,128)(2,1)} copy(bf16[400,8,4,1024]{3,2,1,0:T(4,128)(2,1)} %bitcast.16) | data formatting | bytes 52428800
  25.0 0.0 copy-done.3
  25.0 19.2 %project.1 = (bf16[4,2,128,1024]{3,2,1,0:T(8,128)(2,1)S(1)}, f32[8,128]{1,0:T(8,128)S(1)}, f32[32,1,128]{2,1,0:T(1,128)S(1)}) custom-call(bf16[256,3200]{1,0:T(8,128)(2,1)S(1)} %fusion.5.rows_ref, bf16[3200,4096]{1,0:T(8,128)(2,1)} %bitcast.15, f32[4,1024]{1,0:T(4,128)S(1)} %copy-done.3, bf16[4096,1024]{1,0:T(8,128)(2,1)} %refs_4_.1), custom_call_target="tpu_custom_call" | custom-call | tf_op jit(solution)/shard_map/project/pallas_call | solution.py:360
  44.2 0.0 copy-start.2
  44.2 1.3 copy-done.2
  45.5 0.6 pad_maximum_fusion.stat_ref
  46.1 75.5 %exchange.1 = (bf16[4,4,2,128,1024]{4,3,2,1,0:T(8,128)(2,1)}, f32[32,128]{1,0:T(8,128)}, f32[4,4,8,128]{3,2,1,0:T(8,128)}) custom-call(bf16[4,2,128,1024]{3,2,1,0:T(8,128)(2,1)} %copy-done.2, f32[40,128]{1,0:T(8,128)} %pad_maximum_fusion.stat_ref), custom_call_target="tpu_custom_call" | custom-call | tf_op jit(solution)/shard_map/exchange/pallas_call | solution.py:256
  121.6 1.4 %slice.3 = f32[4,4,2,128]{3,2,1,0:T(2,128)} slice(f32[4,4,8,128]{3,2,1,0:T(8,128)} %get-tuple-element.16), slice={[0:4], [0:4], [0:2], [0:128]} | slice | bytes 32768 | tf_op jit(solution)/shard_map/slice | solution.py:478
  123.1 0.0 copy-start.1
  123.1 12.7 %place.1 = bf16[4096,1024]{1,0:T(8,128)(2,1)} custom-call(s32[32]{0:T(128)} %select_reduce_fusion.source_ref, bf16[32,128,1024]{2,1,0:T(8,128)(2,1)} %bitcast.11, bf16[32,128,1024]{2,1,0:T(8,128)(2,1)} %bitcast.12, bf16[32,128,1024]{2,1,0:T(8,128)(2,1)} %bitcast.13, bf16[32,128,1024]{2,1,0:T(8,128)(2,1)} %bitcast.14, bf16[4096,1024]{1,0:T(8,128)(2,1)} %refs_4_.1, ...), custom_call_target="tpu_custom_call" | custom-call | tf_op jit(solution)/shard_map/place/pallas_call | solution.py:421
  135.8 0.0 copy-done.1
  (3 shorter events, 0.0 us)
Async XLA Ops:
  0.0 0.7 copy-start
  0.0 6.0 %copy-start.4 = (bf16[256,3200]{1,0:T(8,128)(2,1)S(1)}, bf16[256,3200]{1,0:T(8,128)(2,1)}, u32[]{:S(2)}) copy-start(bf16[256,3200]{1,0:T(8,128)(2,1)} %param.9) | copy-start | bytes 4915204
  0.0 6.0 %copy-start.5 = (f32[3200]{0:T(1024)S(1)}, f32[3200]{0:T(1024)}, u32[]{:S(2)}) copy-start(f32[3200]{0:T(1024)} %param.11) | copy-start | bytes 38404
  0.0 6.0 %copy-start.6 = (f32[3200]{0:T(1024)S(1)}, f32[3200]{0:T(1024)}, u32[]{:S(2)}) copy-start(f32[3200]{0:T(1024)} %param.10) | copy-start | bytes 38404
  6.9 18.1 %copy-start.3 = (f32[4,1024]{1,0:T(4,128)S(1)}, f32[4,1024]{1,0:T(4,128)}, u32[]{:S(2)}) copy-start(f32[4,1024]{1,0:T(4,128)} %bias_ref.1) | copy-start | bytes 49156
  44.2 1.3 copy-start.2
  123.1 12.7 %copy-start.1 = (s32[4,32]{1,0:T(4,128)S(1)}, s32[4,32]{1,0:T(4,128)}, u32[]{:S(2)}) copy-start(s32[4,32]{1,0:T(4,128)} %param.17) | copy-start | bytes 1540
